TPU v7x, 128 devices: a whole 4x4x4 slice. The times are simulated.
128 devices in a mesh: narrow: 2 (over core), wide: 64 (over x, y, z).
Axes of the slice: x: 4, y: 4, z: 4, core: 2. Of those that a mesh axis runs over, the one named last changes fastest.
Arguments:
- embeddings: bfloat16 [32768, 256], P(('narrow', 'wide')), may hold values from -6 to 6
- noise: float32 [32768], P(('narrow', 'wide')), may hold values from 0.05 to 0.5
- targets: float32 [32768, 64], P(('narrow', 'wide')), may hold values from -6 to 6
- level_scale: float32 [7], replicated, may hold values from 1.5 to 4
- skeleton: int32 [7, 128, 256], P(None, ('narrow', 'wide')), may hold values from 0 to 32767, as said below
Outputs:
- solution: float32 [32768, 64], P(('narrow', 'wide'))
- fit: float32 [64], replicated
- logdet: float32 [], replicated
Inputs may be any that keep to these rules, and one draw needn't show every extreme that they name: `skeleton`: for each level l (first index l - 1), all devices whose index in narrow+wide has the same quotient by 2**l hold equal rows, and each row holds 256 distinct indices of points of that level-l node.
All inputs are finite; a program needn't handle non-finite values.
Results may differ from a plain program's by a relative error of at most 0.0003.
Values may be sent and summed in bfloat16 or wider, within the bound.
A program may use at most 128 MiB of HBM per device.

v0:
```python
import functools

import jax
import jax.numpy as jnp
from jax import lax
from jax.sharding import Mesh
from jax.sharding import PartitionSpec as P

WIDE = ("wide_0", "wide_1", "wide_2")
NARROW_WIDE = ("narrow", "wide_0", "wide_1", "wide_2")


def for_sending(value):
    return jax.tree.map(lambda a: a.astype(jnp.bfloat16) if a.dtype == jnp.float32 else a, value)


def partner(value, axis, apart):
    mask = 2**apart
    pairs = [(source, source ^ mask) for source in range(lax.axis_size(axis))]
    return lax.ppermute(value, axis, pairs)


def by_axis(value, axes):
    return functools.reduce(lax.psum, axes, value)


def kern(left, right):
    left_sq = jnp.sum(jnp.square(left.astype(jnp.float32)), axis=1)
    right_sq = jnp.sum(jnp.square(right.astype(jnp.float32)), axis=1)
    cross = jnp.dot(left, right.T, preferred_element_type=jnp.float32)
    return jnp.exp(-(left_sq[:, None] + right_sq[None, :] - 2.0 * cross) / left.shape[1])


def block_cholesky(matrix):
    order = matrix.shape[0]
    if order <= 128 or order % 2 != 0:
        return jnp.linalg.cholesky(matrix)
    middle = order // 2
    upper_left = block_cholesky(matrix[:middle, :middle])
    lower_left = jax.scipy.linalg.solve_triangular(
        upper_left, matrix[middle:, :middle].T, lower=True
    ).T
    schur = matrix[middle:, middle:] - jnp.dot(
        lower_left, lower_left.T, precision=lax.Precision.HIGHEST
    )
    lower_right = block_cholesky(schur)
    top_rows = jnp.concatenate(
        [upper_left, jnp.zeros((middle, order - middle), jnp.float32)], axis=1
    )
    bottom_rows = jnp.concatenate([lower_left, lower_right], axis=1)
    return jnp.concatenate([top_rows, bottom_rows], axis=0)


def group_sum(partial_sum, level, wide_bits):
    for bit in range(min(level, wide_bits)):
        partial_sum = partial_sum + partner(for_sending(partial_sum), WIDE, bit).astype(
            partial_sum.dtype
        )
    if level > wide_bits:
        partial_sum = partial_sum + partner(for_sending(partial_sum), "narrow", 0).astype(
            partial_sum.dtype
        )
    return partial_sum


def per_device(embeddings, noise, targets, level_scale, skeleton):
    leaf = embeddings.shape[0]
    rank = skeleton.shape[2]
    levels = skeleton.shape[0]
    wide_bits = lax.axis_size(WIDE).bit_length() - 1
    device = lax.axis_index("narrow") * lax.axis_size(WIDE) + lax.axis_index(WIDE)
    first = device * leaf
    local_index = skeleton[:, 0, :] - first
    inside = (local_index >= 0) & (local_index < leaf)
    fetched = jnp.take(embeddings, jnp.clip(local_index, 0, leaf - 1), axis=0)
    centers = jnp.where(inside[:, :, None], fetched, jnp.zeros_like(fetched))
    for bit in range(wide_bits):
        pending = centers[bit:]
        centers = centers.at[bit:].set(pending + partner(pending, WIDE, bit))
    topmost = centers[levels - 1 :]
    centers = centers.at[levels - 1 :].set(topmost + partner(topmost, "narrow", 0))
    gram = kern(embeddings, embeddings) + jnp.diag(noise)
    chol = block_cholesky(gram)
    bases = []
    for level in range(levels):
        bases.append(kern(embeddings, centers[level]) * jnp.sqrt(level_scale[level] / rank))
    stacked = jnp.concatenate(bases + [targets], axis=1)
    solved = jax.scipy.linalg.cho_solve((chol, True), stacked)
    det_term = 2.0 * jnp.sum(jnp.log(jnp.diagonal(chol)))
    for level in range(levels):
        start = level * rank
        partial_sum = jnp.dot(bases[level].T, solved[:, start:], precision=lax.Precision.HIGHEST)
        summed = group_sum(partial_sum, level + 1, wide_bits)
        cap = jnp.eye(rank, dtype=jnp.float32) + summed[:, :rank]
        capchol = block_cholesky(cap)
        coef = jax.scipy.linalg.cho_solve((capchol, True), summed[:, rank:])
        update = jnp.dot(solved[:, start : start + rank], coef, precision=lax.Precision.HIGHEST)
        solved = jnp.concatenate(
            [solved[:, : start + rank], solved[:, start + rank :] - update], axis=1
        )
        det_term = det_term + 2.0 * jnp.sum(jnp.log(jnp.diagonal(capchol))) / 2 ** (level + 1)
    solution = solved[:, levels * rank :]
    fit_term = jnp.sum(targets * solution, axis=0)
    fit_total, det_total = (by_axis(fit_term, NARROW_WIDE), by_axis(det_term, NARROW_WIDE))
    npoints = leaf * lax.axis_size("narrow") * lax.axis_size(WIDE)
    return (solution, fit_total / npoints, det_total / npoints)


def solution(mesh):
    finer = Mesh(
        mesh.devices.reshape(mesh.shape["narrow"], 4, 4, 4),
        ("narrow", "wide_0", "wide_1", "wide_2"),
    )
    return jax.shard_map(
        per_device,
        mesh=finer,
        in_specs=(
            P(NARROW_WIDE, None),
            P(NARROW_WIDE),
            P(NARROW_WIDE, None),
            P(),
            P(None, NARROW_WIDE, None),
        ),
        out_specs=(P(NARROW_WIDE, None), P(), P()),
        check_vma=False,
    )
```

profile of v0, /device:TPU:1, one launch (start us, length us, event | category | flops | bytes accessed | tf_op | source)
XLA Modules:
  0.0 980.6 jit_solution(16074617090839990940)
XLA Ops:
  11.0 11.7 %cholesky.254 = f32[128,128]{1,0:T(8,128)S(1)} custom-call(f32[128,128]{1,0:T(8,128)S(1)} %fusion.153), custom_call_target="Cholesky" | custom-call | tf_op jit(solution)/shard_map/jit(cholesky)/cholesky | solution.py:37
  50.7 11.7 %cholesky.265 = f32[128,128]{1,0:T(8,128)S(1)} custom-call(f32[128,128]{1,0:T(8,128)S(1)} %fusion.151), custom_call_target="Cholesky" | custom-call | tf_op jit(solution)/shard_map/jit(cholesky)/cholesky | solution.py:37
  85.2 19.7 %custom-call.61 = f32[2,128,128]{1,2,0:T(8,128)S(1)} custom-call(f32[2,128,128]{2,1,0:T(8,128)S(1)} %get-tuple-element.104), custom_call_target="InvertDiagBlocksLowerTriangular" | custom-call | tf_op jit(solution)/shard_map/jit(_cho_solve)/triangular_solve | solution.py:88
  138.7 21.6 %collective-permute-done.7 = bf16[256,1856]{0,1:T(8,128)(2,1)} collective-permute-done((bf16[256,1856]{0,1:T(8,128)(2,1)S(1)}, bf16[256,1856]{0,1:T(8,128)(2,1)}, u32[]{:S(2)}, u32[]{:S(2)}) %collective-permute-start.7) | collective-permute-done | bytes 950304 | tf_op jit(solution)/shard_map/ppermute | solution.py:20
  163.7 11.7 %cholesky.276 = f32[128,128]{1,0:T(8,128)S(1)} custom-call(f32[128,128]{1,0:T(8,128)S(1)} %fusion.150), custom_call_target="Cholesky" | custom-call | tf_op jit(solution)/shard_map/jit(cholesky)/cholesky | solution.py:37
  187.5 11.7 %cholesky.287 = f32[128,128]{1,0:T(8,128)S(1)} custom-call(f32[128,128]{1,0:T(8,128)S(1)} %fusion.148), custom_call_target="Cholesky" | custom-call | tf_op jit(solution)/shard_map/jit(cholesky)/cholesky | solution.py:37
  206.0 19.7 %custom-call.62 = f32[2,128,128]{1,2,0:T(8,128)S(1)} custom-call(f32[2,128,128]{2,1,0:T(8,128)S(1)} %get-tuple-element.112), custom_call_target="InvertDiagBlocksLowerTriangular" | custom-call | tf_op jit(solution)/shard_map/jit(_cho_solve)/triangular_solve | solution.py:96
  237.4 17.8 %collective-permute-done.8 = bf16[256,1600]{0,1:T(8,128)(2,1)S(1)} collective-permute-done((bf16[256,1600]{0,1:T(8,128)(2,1)S(1)}, bf16[256,1600]{0,1:T(8,128)(2,1)S(1)}, u32[]{:S(2)}, u32[]{:S(2)}) %collective-permute-start.8) | collective-permute-done | bytes 819232 | tf_op jit(solution)/shard_map/ppermute | solution.py:20
  257.3 18.9 %collective-permute-done.9 = bf16[256,1600]{0,1:T(8,128)(2,1)} collective-permute-done((bf16[256,1600]{0,1:T(8,128)(2,1)}, bf16[256,1600]{0,1:T(8,128)(2,1)}, u32[]{:S(2)}, u32[]{:S(2)}) %collective-permute-start.9) | collective-permute-done | bytes 819232 | tf_op jit(solution)/shard_map/ppermute | solution.py:20
  279.1 11.7 %cholesky.298 = f32[128,128]{1,0:T(8,128)S(1)} custom-call(f32[128,128]{1,0:T(8,128)S(1)} %fusion.147), custom_call_target="Cholesky" | custom-call | tf_op jit(solution)/shard_map/jit(cholesky)/cholesky | solution.py:37
  303.6 12.5 %cholesky.309 = f32[128,128]{1,0:T(8,128)S(1)} custom-call(f32[128,128]{1,0:T(8,128)} %fusion.145), custom_call_target="Cholesky" | custom-call | tf_op jit(solution)/shard_map/jit(cholesky)/cholesky | solution.py:37
  326.8 21.1 %custom-call.63 = f32[2,128,128]{1,2,0:T(8,128)} custom-call(f32[2,128,128]{2,1,0:T(8,128)} %get-tuple-element.120), custom_call_target="InvertDiagBlocksLowerTriangular" | custom-call | tf_op jit(solution)/shard_map/jit(_cho_solve)/triangular_solve | solution.py:96
  357.3 13.3 %collective-permute-done.10 = bf16[256,1344]{0,1:T(8,128)(2,1)S(1)} collective-permute-done((bf16[256,1344]{0,1:T(8,128)(2,1)S(1)}, bf16[256,1344]{0,1:T(8,128)(2,1)S(1)}, u32[]{:S(2)}, u32[]{:S(2)}) %collective-permute-start.10) | collective-permute-done | bytes 688160 | tf_op jit(solution)/shard_map/ppermute | solution.py:20
  371.5 13.3 %collective-permute-done.11 = bf16[256,1344]{0,1:T(8,128)(2,1)S(1)} collective-permute-done((bf16[256,1344]{0,1:T(8,128)(2,1)S(1)}, bf16[256,1344]{0,1:T(8,128)(2,1)S(1)}, u32[]{:S(2)}, u32[]{:S(2)}) %collective-permute-start.11) | collective-permute-done | bytes 688160 | tf_op jit(solution)/shard_map/ppermute | solution.py:20
  386.5 11.5 %collective-permute-done.12 = bf16[256,1344]{0,1:T(8,128)(2,1)} collective-permute-done((bf16[256,1344]{0,1:T(8,128)(2,1)}, bf16[256,1344]{0,1:T(8,128)(2,1)}, u32[]{:S(2)}, u32[]{:S(2)}) %collective-permute-start.12) | collective-permute-done | bytes 688160 | tf_op jit(solution)/shard_map/ppermute | solution.py:20
  401.0 11.7 %cholesky.320 = f32[128,128]{1,0:T(8,128)S(1)} custom-call(f32[128,128]{1,0:T(8,128)S(1)} %fusion.144), custom_call_target="Cholesky" | custom-call | tf_op jit(solution)/shard_map/jit(cholesky)/cholesky | solution.py:37
  425.5 11.7 %cholesky.331 = f32[128,128]{1,0:T(8,128)S(1)} custom-call(f32[128,128]{1,0:T(8,128)S(1)} %fusion.142), custom_call_target="Cholesky" | custom-call | tf_op jit(solution)/shard_map/jit(cholesky)/cholesky | solution.py:37
  444.2 19.7 %custom-call.64 = f32[2,128,128]{1,2,0:T(8,128)S(1)} custom-call(f32[2,128,128]{2,1,0:T(8,128)S(1)} %get-tuple-element.128), custom_call_target="InvertDiagBlocksLowerTriangular" | custom-call | tf_op jit(solution)/shard_map/jit(_cho_solve)/triangular_solve | solution.py:96
  484.3 11.9 %collective-permute-done.14 = bf16[256,1088]{0,1:T(8,128)(2,1)S(1)} collective-permute-done((bf16[256,1088]{0,1:T(8,128)(2,1)S(1)}, bf16[256,1088]{0,1:T(8,128)(2,1)S(1)}, u32[]{:S(2)}, u32[]{:S(2)}) %collective-permute-start.14) | collective-permute-done | bytes 557088 | tf_op jit(solution)/shard_map/ppermute | solution.py:20
  519.9 11.7 %cholesky.342 = f32[128,128]{1,0:T(8,128)S(1)} custom-call(f32[128,128]{1,0:T(8,128)S(1)} %fusion.141), custom_call_target="Cholesky" | custom-call | tf_op jit(solution)/shard_map/jit(cholesky)/cholesky | solution.py:37
  543.8 11.7 %cholesky.353 = f32[128,128]{1,0:T(8,128)S(1)} custom-call(f32[128,128]{1,0:T(8,128)S(1)} %fusion.139), custom_call_target="Cholesky" | custom-call | tf_op jit(solution)/shard_map/jit(cholesky)/cholesky | solution.py:37
  561.5 19.7 %custom-call.65 = f32[2,128,128]{1,2,0:T(8,128)S(1)} custom-call(f32[2,128,128]{2,1,0:T(8,128)S(1)} %get-tuple-element.136), custom_call_target="InvertDiagBlocksLowerTriangular" | custom-call | tf_op jit(solution)/shard_map/jit(_cho_solve)/triangular_solve | solution.py:96
  634.7 11.7 %cholesky.364 = f32[128,128]{1,0:T(8,128)S(1)} custom-call(f32[128,128]{1,0:T(8,128)S(1)} %fusion.138), custom_call_target="Cholesky" | custom-call | tf_op jit(solution)/shard_map/jit(cholesky)/cholesky | solution.py:37
  658.5 11.7 %cholesky.375 = f32[128,128]{1,0:T(8,128)S(1)} custom-call(f32[128,128]{1,0:T(8,128)S(1)} %fusion.136), custom_call_target="Cholesky" | custom-call | tf_op jit(solution)/shard_map/jit(cholesky)/cholesky | solution.py:37
  676.4 19.7 %custom-call.66 = f32[2,128,128]{1,2,0:T(8,128)S(1)} custom-call(f32[2,128,128]{2,1,0:T(8,128)S(1)} %get-tuple-element.144), custom_call_target="InvertDiagBlocksLowerTriangular" | custom-call | tf_op jit(solution)/shard_map/jit(_cho_solve)/triangular_solve | solution.py:96
  746.4 11.7 %cholesky.386 = f32[128,128]{1,0:T(8,128)S(1)} custom-call(f32[128,128]{1,0:T(8,128)S(1)} %fusion.135), custom_call_target="Cholesky" | custom-call | tf_op jit(solution)/shard_map/jit(cholesky)/cholesky | solution.py:37
  770.3 11.7 %cholesky.397 = f32[128,128]{1,0:T(8,128)S(1)} custom-call(f32[128,128]{1,0:T(8,128)S(1)} %fusion.133), custom_call_target="Cholesky" | custom-call | tf_op jit(solution)/shard_map/jit(cholesky)/cholesky | solution.py:37
  787.9 19.7 %custom-call.67 = f32[2,128,128]{1,2,0:T(8,128)S(1)} custom-call(f32[2,128,128]{2,1,0:T(8,128)S(1)} %get-tuple-element.152), custom_call_target="InvertDiagBlocksLowerTriangular" | custom-call | tf_op jit(solution)/shard_map/jit(_cho_solve)/triangular_solve | solution.py:96
  853.3 23.2 %collective-permute-start.34 = (bf16[256,320]{0,1:T(8,128)(2,1)S(1)}, bf16[256,320]{0,1:T(8,128)(2,1)S(1)}, u32[]{:S(2)}, u32[]{:S(2)}) collective-permute-start(bf16[256,320]{0,1:T(8,128)(2,1)S(1)} %fusion.118), channel_id=1, source_target_pairs={{0,64},{64,0},{1,65},{65,1},{2,66},{66,2},{3,67},{67,3},{4,68},{68... | collective-permute-start | bytes 491528 | tf_op jit(solution)/shard_map/ppermute | solution.py:20
  882.1 11.7 %cholesky.408 = f32[128,128]{1,0:T(8,128)S(1)} custom-call(f32[128,128]{1,0:T(8,128)S(1)} %fusion.132), custom_call_target="Cholesky" | custom-call | tf_op jit(solution)/shard_map/jit(cholesky)/cholesky | solution.py:37
  905.9 11.7 %cholesky.419 = f32[128,128]{1,0:T(8,128)S(1)} custom-call(f32[128,128]{1,0:T(8,128)S(1)} %fusion.130), custom_call_target="Cholesky" | custom-call | tf_op jit(solution)/shard_map/jit(cholesky)/cholesky | solution.py:37
  926.6 19.8 %custom-call.68 = f32[2,128,128]{1,2,0:T(8,128)S(1)} custom-call(f32[2,128,128]{2,1,0:T(8,128)S(1)} %get-tuple-element.160), custom_call_target="InvertDiagBlocksLowerTriangular" | custom-call | tf_op jit(solution)/shard_map/jit(_cho_solve)/triangular_solve | solution.py:96
  (519 shorter events, 523.2 us)
Async XLA Ops:
  7.9 22.6 %collective-permute-start = (bf16[7,256,256]{2,1,0:T(8,128)(2,1)S(1)}, bf16[7,256,256]{2,1,0:T(8,128)(2,1)S(1)}, u32[]{:S(2)}, u32[]{:S(2)}) collective-permute-start(bf16[7,256,256]{2,1,0:T(8,128)(2,1)S(1)} %select_select_fusion), channel_id=1, source_target_pairs={{0,1},{1,0},{2,3},{3,2},{4,5},{5,4},{6,7},{7,6},{8,9},{9,8},{10,11... | collective-permute-start | bytes 2752520 | tf_op jit(solution)/shard_map/ppermute | solution.py:20
  31.2 31.3 %collective-permute-start.1 = (bf16[6,256,256]{2,1,0:T(8,128)(2,1)S(1)}, bf16[6,256,256]{2,1,0:T(8,128)(2,1)S(1)}, u32[]{:S(2)}, u32[]{:S(2)}) collective-permute-start(bf16[6,256,256]{2,1,0:T(8,128)(2,1)S(1)} %slice.794), channel_id=1, source_target_pairs={{0,2},{1,3},{2,0},{3,1},{4,6},{5,7},{6,4},{7,5},{8,10},{9,11},{10,... | collective-permute-start | bytes 2359304 | tf_op jit(solution)/shard_map/ppermute | solution.py:20
  63.0 14.6 %collective-permute-start.2 = (bf16[5,256,256]{2,1,0:T(8,128)(2,1)S(1)}, bf16[5,256,256]{2,1,0:T(8,128)(2,1)S(1)}, u32[]{:S(2)}, u32[]{:S(2)}) collective-permute-start(bf16[5,256,256]{2,1,0:T(8,128)(2,1)S(1)} %slice.795), channel_id=1, source_target_pairs={{0,4},{1,5},{2,6},{3,7},{4,0},{5,1},{6,2},{7,3},{8,12},{9,13},{10,... | collective-permute-start | bytes 1966088 | tf_op jit(solution)/shard_map/ppermute | solution.py:20
  77.8 27.1 %collective-permute-start.3 = (bf16[4,256,256]{2,1,0:T(8,128)(2,1)S(1)}, bf16[4,256,256]{2,1,0:T(8,128)(2,1)S(1)}, u32[]{:S(2)}, u32[]{:S(2)}) collective-permute-start(bf16[4,256,256]{2,1,0:T(8,128)(2,1)S(1)} %slice.796), channel_id=1, source_target_pairs={{0,8},{1,9},{2,10},{3,11},{4,12},{5,13},{6,14},{7,15},{8,0},{9,1},... | collective-permute-start | bytes 1572872 | tf_op jit(solution)/shard_map/ppermute | solution.py:20
  105.1 7.8 collective-permute-start.4
  112.9 8.0 collective-permute-start.5
  137.5 22.7 %collective-permute-start.7 = (bf16[256,1856]{0,1:T(8,128)(2,1)S(1)}, bf16[256,1856]{0,1:T(8,128)(2,1)}, u32[]{:S(2)}, u32[]{:S(2)}) collective-permute-start(bf16[256,1856]{0,1:T(8,128)(2,1)S(1)} %get-tuple-element.385), channel_id=1, source_target_pairs={{0,1},{1,0},{2,3},{3,2},{4,5},{5,4},{6,7},{7,6},{8,9},{9,8},{10,11... | collective-permute-start | bytes 2850824 | tf_op jit(solution)/shard_map/ppermute | solution.py:20
  236.6 18.7 %collective-permute-start.8 = (bf16[256,1600]{0,1:T(8,128)(2,1)S(1)}, bf16[256,1600]{0,1:T(8,128)(2,1)S(1)}, u32[]{:S(2)}, u32[]{:S(2)}) collective-permute-start(bf16[256,1600]{0,1:T(8,128)(2,1)S(1)} %get-tuple-element.387), channel_id=1, source_target_pairs={{0,1},{1,0},{2,3},{3,2},{4,5},{5,4},{6,7},{7,6},{8,9},{9,8},{10,11... | collective-permute-start | bytes 2457608 | tf_op jit(solution)/shard_map/ppermute | solution.py:20
  256.4 19.7 %collective-permute-start.9 = (bf16[256,1600]{0,1:T(8,128)(2,1)}, bf16[256,1600]{0,1:T(8,128)(2,1)}, u32[]{:S(2)}, u32[]{:S(2)}) collective-permute-start(bf16[256,1600]{0,1:T(8,128)(2,1)} %fusion.55), channel_id=1, source_target_pairs={{0,2},{1,3},{2,0},{3,1},{4,6},{5,7},{6,4},{7,5},{8,10},{9,11},{10,... | collective-permute-start | bytes 2457608 | tf_op jit(solution)/shard_map/ppermute | solution.py:20
  356.5 14.1 %collective-permute-start.10 = (bf16[256,1344]{0,1:T(8,128)(2,1)S(1)}, bf16[256,1344]{0,1:T(8,128)(2,1)S(1)}, u32[]{:S(2)}, u32[]{:S(2)}) collective-permute-start(bf16[256,1344]{0,1:T(8,128)(2,1)S(1)} %get-tuple-element.389), channel_id=1, source_target_pairs={{0,1},{1,0},{2,3},{3,2},{4,5},{5,4},{6,7},{7,6},{8,9},{9,8},{10,11... | collective-permute-start | bytes 2064392 | tf_op jit(solution)/shard_map/ppermute | solution.py:20
  370.8 14.0 %collective-permute-start.11 = (bf16[256,1344]{0,1:T(8,128)(2,1)S(1)}, bf16[256,1344]{0,1:T(8,128)(2,1)S(1)}, u32[]{:S(2)}, u32[]{:S(2)}) collective-permute-start(bf16[256,1344]{0,1:T(8,128)(2,1)S(1)} %fusion.59), channel_id=1, source_target_pairs={{0,2},{1,3},{2,0},{3,1},{4,6},{5,7},{6,4},{7,5},{8,10},{9,11},{10,... | collective-permute-start | bytes 2064392 | tf_op jit(solution)/shard_map/ppermute | solution.py:20
  386.0 12.0 %collective-permute-start.12 = (bf16[256,1344]{0,1:T(8,128)(2,1)}, bf16[256,1344]{0,1:T(8,128)(2,1)}, u32[]{:S(2)}, u32[]{:S(2)}) collective-permute-start(bf16[256,1344]{0,1:T(8,128)(2,1)} %fusion.81), channel_id=1, source_target_pairs={{0,4},{1,5},{2,6},{3,7},{4,0},{5,1},{6,2},{7,3},{8,12},{9,13},{10,... | collective-permute-start | bytes 2064392 | tf_op jit(solution)/shard_map/ppermute | solution.py:20
  470.4 8.5 collective-permute-start.13
  479.0 17.2 %collective-permute-start.14 = (bf16[256,1088]{0,1:T(8,128)(2,1)S(1)}, bf16[256,1088]{0,1:T(8,128)(2,1)S(1)}, u32[]{:S(2)}, u32[]{:S(2)}) collective-permute-start(bf16[256,1088]{0,1:T(8,128)(2,1)S(1)} %fusion.68), channel_id=1, source_target_pairs={{0,2},{1,3},{2,0},{3,1},{4,6},{5,7},{6,4},{7,5},{8,10},{9,11},{10,... | collective-permute-start | bytes 1671176 | tf_op jit(solution)/shard_map/ppermute | solution.py:20
  496.4 8.9 collective-permute-start.15
  506.4 11.0 %collective-permute-start.16 = (bf16[256,1088]{0,1:T(8,128)(2,1)}, bf16[256,1088]{0,1:T(8,128)(2,1)}, u32[]{:S(2)}, u32[]{:S(2)}) collective-permute-start(bf16[256,1088]{0,1:T(8,128)(2,1)} %fusion.69), channel_id=1, source_target_pairs={{0,8},{1,9},{2,10},{3,11},{4,12},{5,13},{6,14},{7,15},{8,0},{9,1},... | collective-permute-start | bytes 1671176 | tf_op jit(solution)/shard_map/ppermute | solution.py:20
  587.8 7.1 collective-permute-start.17
  595.0 10.4 %collective-permute-start.18 = (bf16[256,832]{0,1:T(8,128)(2,1)S(1)}, bf16[256,832]{0,1:T(8,128)(2,1)S(1)}, u32[]{:S(2)}, u32[]{:S(2)}) collective-permute-start(bf16[256,832]{0,1:T(8,128)(2,1)S(1)} %fusion.76), channel_id=1, source_target_pairs={{0,2},{1,3},{2,0},{3,1},{4,6},{5,7},{6,4},{7,5},{8,10},{9,11},{10,... | collective-permute-start | bytes 1277960 | tf_op jit(solution)/shard_map/ppermute | solution.py:20
  605.5 7.1 collective-permute-start.19
  612.7 9.4 collective-permute-start.20
  623.8 7.5 collective-permute-start.21
  702.2 5.7 collective-permute-start.22
  707.9 9.8 collective-permute-start.23
  717.8 5.9 collective-permute-start.24
  723.9 7.5 collective-permute-start.25
  731.6 5.9 collective-permute-start.26
  737.6 7.5 collective-permute-start.27
  815.7 5.8 collective-permute-start.29
  825.8 8.4 collective-permute-start.31
  834.3 8.8 collective-permute-start.32
  843.2 10.0 %collective-permute-start.33 = (bf16[256,320]{0,1:T(8,128)(2,1)S(1)}, bf16[256,320]{0,1:T(8,128)(2,1)S(1)}, u32[]{:S(2)}, u32[]{:S(2)}) collective-permute-start(bf16[256,320]{0,1:T(8,128)(2,1)S(1)} %fusion.113), channel_id=1, source_target_pairs={{0,32},{1,33},{2,34},{3,35},{4,36},{5,37},{6,38},{7,39},{8,40},{9,... | collective-permute-start | bytes 491528 | tf_op jit(solution)/shard_map/ppermute | solution.py:20
  853.3 28.5 %collective-permute-start.34 = (bf16[256,320]{0,1:T(8,128)(2,1)S(1)}, bf16[256,320]{0,1:T(8,128)(2,1)S(1)}, u32[]{:S(2)}, u32[]{:S(2)}) collective-permute-start(bf16[256,320]{0,1:T(8,128)(2,1)S(1)} %fusion.118), channel_id=1, source_target_pairs={{0,64},{64,0},{1,65},{65,1},{2,66},{66,2},{3,67},{67,3},{4,68},{68... | collective-permute-start | bytes 491528 | tf_op jit(solution)/shard_map/ppermute | solution.py:20
  (34 other events, 275.4 us)
where the time goes:
time: 992 us; the launch traced here: 981 us
  other arithmetic  480 us (48%)
  waiting for transfers between devices  229 us (23%)
  starting transfers between devices  89.7 us (9%)
  local copies, waits for them, and re-layouts  72.3 us (7%)
  matrix products  63.7 us (6%)
  blocking collectives  28.5 us (3%)
  between operations  14.9 us (2%)
    ppermute x35, waiting for transfers between devices, partner(): return lax.ppermute(value, axis, pairs)  229 us
    another operation x48, other arithmetic, block_cholesky(): return jnp.linalg.cholesky(matrix)  200 us
    another operation x7, other arithmetic, per_device(): coef = jax.scipy.linalg.cho_solve((capchol, True), summed[:, rank:])  139 us
    ppermute x35, starting transfers between devices, partner(): return lax.ppermute(value, axis, pairs)  89.7 us
    another operation x16, other arithmetic, block_cholesky(): jax.scipy.linalg.solve_triangular(upper_left, matrix[middle:, :middle].T,...  84.4 us
    another operation x80, local copies, waits for them, and re-layouts  36.4 us
    another operation x42, matrix products, per_device(): coef = jax.scipy.linalg.cho_solve((capchol, True), summed[:, rank:])  29.8 us
    psum x4, blocking collectives, by_axis(): return functools.reduce(lax.psum, axes, value)  28.5 us
  transfers between devices with their start and end apart: 35, of which 28 were waited for; matrix products, arithmetic and copies ran while one was open for 9% of the time, Pallas kernels for 0%

commit v1 on v0

v1 whole, which is shorter than its diff:
```python
import functools

import jax
import jax.numpy as jnp
from jax import lax
from jax.experimental import pallas as pl
from jax.experimental.pallas import tpu as pltpu
from jax.sharding import PartitionSpec as P

NARROW_WIDE = ("narrow", "wide")
MESH = pl.DeviceIdType.MESH
EXACT = lax.Precision.HIGHEST
CLOSE = lax.Precision.HIGH
LANES = 128
VMEM = pltpu.VMEM


def exact_dot(left, right):
    return jnp.dot(left, right, precision=EXACT, preferred_element_type=jnp.float32)


def unit(k):
    return jnp.where(lax.broadcasted_iota(jnp.int32, (8, LANES), 0) == k, 1.0, 0.0)


def inverse8(cols):
    cols = list(cols)
    logs = jnp.zeros((1, LANES), jnp.float32)
    for k in range(0, 8, 2):
        a, e = cols[k][k : k + 1], cols[k][k + 1 : k + 2]
        b, c = cols[k + 1][k : k + 1], cols[k + 1][k + 1 : k + 2]
        det = a * c - b * e
        inv = 1.0 / det
        logs = logs + jnp.log(det)
        ai, bi, ci, ei = a * inv, b * inv, c * inv, e * inv
        first, second = cols[k] - unit(k), cols[k + 1] - unit(k + 1)
        m0 = first * ci - second * ei
        m1 = second * ai - first * bi
        for j in range(8):
            if j == k:
                cols[j] = unit(k) - m0
            elif j == k + 1:
                cols[j] = unit(k + 1) - m1
            else:
                cols[j] = cols[j] - m0 * cols[j][k : k + 1] - m1 * cols[j][k + 1 : k + 2]
    return cols, logs


def inverse128(load, store, spread_ref):
    lane = lax.broadcasted_iota(jnp.int32, (8, LANES), 1)
    sub = lax.broadcasted_iota(jnp.int32, (8, LANES), 0)
    tiles = LANES // 8
    state = [load(q) for q in range(tiles)]
    total = jnp.zeros((1, LANES), jnp.float32)
    for p in range(tiles):
        cols = [
            [jnp.broadcast_to(state[q][:, 8 * p + j : 8 * p + j + 1], (8, LANES)) for j in range(8)]
            for q in range(tiles)
        ]
        for j in range(8):
            spread_ref[j] = cols[p][j]
        block, logs = inverse8([spread_ref[j] for j in range(8)])
        total = total + logs
        inside = (lane >= 8 * p) & (lane < 8 * p + 8)
        pivot_rows = jnp.where(inside, jnp.where(lane - 8 * p == sub, 1.0, 0.0), state[p])
        scaled = block[0] * pivot_rows[0:1]
        for j in range(1, 8):
            scaled = scaled + block[j] * pivot_rows[j : j + 1]
        rows = [jnp.broadcast_to(scaled[j : j + 1], (8, LANES)) for j in range(8)]
        for q in range(tiles):
            if q == p:
                state[q] = scaled
            else:
                rest = jnp.where(inside, 0.0, state[q])
                for j in range(8):
                    rest = rest - cols[q][j] * rows[j]
                state[q] = rest
    for q in range(tiles):
        store(q, state[q])
    return total


def inverse_kernel(matrix_ref, out_ref, log_ref, spread_ref):
    out_ref[...] = matrix_ref[...]
    log_ref[...] = jnp.zeros_like(log_ref)
    half = out_ref.shape[0] // 2

    def step(j, carry):
        here = pl.ds(pl.multiple_of(j * half, half), half)
        there = pl.ds(pl.multiple_of((1 - j) * half, half), half)

        def rows(q):
            return pl.ds(pl.multiple_of(j * half + 8 * q, 8), 8)

        def store(q, value):
            out_ref[rows(q), here] = value

        log_ref[0:1, :] += inverse128(lambda q: out_ref[rows(q), here], store, spread_ref)
        inv = out_ref[here, here]
        scaled = exact_dot(inv, out_ref[here, there])
        below = out_ref[there, here]
        out_ref[there, there] = out_ref[there, there] - exact_dot(below, scaled)
        out_ref[there, here] = -exact_dot(below, inv)
        out_ref[here, there] = scaled
        return carry

    lax.fori_loop(0, 2, step, 0)


def spd_inverse(matrix):
    order = matrix.shape[0]
    assert order == 2 * LANES
    inverse, logs = pl.pallas_call(
        inverse_kernel,
        out_shape=(
            jax.ShapeDtypeStruct((order, order), jnp.float32),
            jax.ShapeDtypeStruct((8, LANES), jnp.float32),
        ),
        in_specs=[pl.BlockSpec(memory_space=VMEM)],
        out_specs=(pl.BlockSpec(memory_space=VMEM), pl.BlockSpec(memory_space=VMEM)),
        scratch_shapes=[VMEM((8, 8, LANES), jnp.float32)],
        cost_estimate=pl.CostEstimate(flops=60_000_000, bytes_accessed=600_000, transcendentals=512),
        name="spd_inverse",
    )(matrix)
    return inverse, logs[0, 0]


def near_far(level):
    near = min(2**level, 16)
    return near, 2**level // near


def near_peer(near, k):
    narrow, wide = lax.axis_index("narrow"), lax.axis_index("wide")
    here = lax.rem(wide, near)
    peer = lax.rem(here + k, near)
    return here, peer, (narrow, wide - here + peer)


def far_peer(far, k):
    narrow, wide = lax.axis_index("narrow"), lax.axis_index("wide")
    slab, inner = lax.div(wide, 16), lax.rem(wide, 16)
    index = slab if far <= 4 else narrow * 4 + slab
    here = lax.rem(index, far)
    peer = index - here + lax.rem(here + k, far)
    if far <= 4:
        return here, (narrow, peer * 16 + inner)
    return here, (lax.div(peer, 4), lax.rem(peer, 4) * 16 + inner)


def remote(src, dst, send_sem, recv_sem, device):
    return pltpu.make_async_remote_copy(
        src_ref=src, dst_ref=dst, send_sem=send_sem, recv_sem=recv_sem, device_id=device, device_id_type=MESH
    )


def greet(near, far):
    barrier = pltpu.get_barrier_semaphore()
    for k in range(1, near):
        pl.semaphore_signal(barrier, inc=1, device_id=near_peer(near, k)[2], device_id_type=MESH)
    for k in range(1, far):
        pl.semaphore_signal(barrier, inc=1, device_id=far_peer(far, k)[1], device_id_type=MESH)
    pl.semaphore_wait(barrier, near + far - 2)


def node_sum_kernel(near, far, part_ref, out_ref, landed, passed, own, *sems):
    rows = part_ref.shape[0] // near

    def block(index):
        return pl.ds(pl.multiple_of(index * rows, rows), rows)

    scatter_send, scatter_recv, gather_send, gather_recv = sems[:4]
    greet(near, far)
    here = near_peer(near, 0)[0]
    copies = []
    for k in range(1, near):
        _, peer, device = near_peer(near, k)
        copies.append(
            remote(part_ref.at[block(peer)], landed.at[k - 1], scatter_send.at[k - 1], scatter_recv.at[k - 1], device)
        )
        copies[-1].start()
    total = part_ref[block(here)].astype(jnp.float32)
    for k in range(1, near):
        copies[k - 1].wait()
        total = total + landed[k - 1].astype(jnp.float32)
    if far > 1:
        far_send, far_recv = sems[4:]
        own[...] = total.astype(jnp.bfloat16)
        copies = []
        for k in range(1, far):
            copies.append(
                remote(own, passed.at[k - 1], far_send.at[k - 1], far_recv.at[k - 1], far_peer(far, k)[1])
            )
            copies[-1].start()
        total = own[...].astype(jnp.float32)
        for k in range(1, far):
            copies[k - 1].wait()
            total = total + passed[k - 1].astype(jnp.float32)
    out_ref[block(here)] = total.astype(jnp.bfloat16)
    copies = []
    for k in range(1, near):
        device = near_peer(near, k)[2]
        mine = out_ref.at[block(here)]
        copies.append(remote(mine, mine, gather_send.at[k - 1], gather_recv.at[k - 1], device))
        copies[-1].start()
    for copy in copies:
        copy.wait()


def node_sum(part, level):
    near, far = near_far(level)
    order, columns = part.shape
    rows = order // near
    dma = pltpu.SemaphoreType.DMA
    sems = [dma((near - 1,)) for _ in range(4)] + ([dma((far - 1,)) for _ in range(2)] if far > 1 else [])
    return pl.pallas_call(
        functools.partial(node_sum_kernel, near, far),
        out_shape=jax.ShapeDtypeStruct((order, columns), jnp.bfloat16),
        in_specs=[pl.BlockSpec(memory_space=VMEM)],
        out_specs=pl.BlockSpec(memory_space=VMEM),
        scratch_shapes=[
            VMEM((near - 1, rows, columns), jnp.bfloat16),
            VMEM((max(far - 1, 1), rows, columns), jnp.bfloat16),
            VMEM((rows, columns), jnp.bfloat16),
            *sems,
        ],
        compiler_params=pltpu.CompilerParams(collective_id=level, has_side_effects=True),
        name=f"node_sum_{level}",
    )(part)


def whole_sum_kernel(near, far, part_ref, out_ref, landed, passed, own, near_send, near_recv, far_send, far_recv):
    greet(near, far)
    here = near_peer(near, 0)[0]
    landed[here] = part_ref[...]
    copies = []
    for k in range(1, near):
        copies.append(
            remote(part_ref, landed.at[here], near_send.at[k - 1], near_recv.at[k - 1], near_peer(near, k)[2])
        )
        copies[-1].start()
    for copy in copies:
        copy.wait()
    total = landed[0]
    for k in range(1, near):
        total = total + landed[k]
    own[...] = total
    index = far_peer(far, 0)[0]
    passed[index] = total
    copies = []
    for k in range(1, far):
        copies.append(remote(own, passed.at[index], far_send.at[k - 1], far_recv.at[k - 1], far_peer(far, k)[1]))
        copies[-1].start()
    for copy in copies:
        copy.wait()
    total = passed[0]
    for k in range(1, far):
        total = total + passed[k]
    out_ref[...] = total


def whole_sum(part):
    near, far = near_far(7)
    dma = pltpu.SemaphoreType.DMA
    return pl.pallas_call(
        functools.partial(whole_sum_kernel, near, far),
        out_shape=jax.ShapeDtypeStruct(part.shape, jnp.float32),
        in_specs=[pl.BlockSpec(memory_space=VMEM)],
        out_specs=pl.BlockSpec(memory_space=VMEM),
        scratch_shapes=[
            VMEM((near, *part.shape), jnp.float32),
            VMEM((far, *part.shape), jnp.float32),
            VMEM(part.shape, jnp.float32),
            dma((near - 1,)),
            dma((near - 1,)),
            dma((far - 1,)),
            dma((far - 1,)),
        ],
        compiler_params=pltpu.CompilerParams(collective_id=8, has_side_effects=True),
        name="whole_sum",
    )(part)


def partner(value, axis, apart):
    mask = 2**apart
    pairs = [(source, source ^ mask) for source in range(lax.axis_size(axis))]
    return lax.ppermute(value, axis, pairs)


def kern(left, right):
    left_sq = jnp.sum(jnp.square(left.astype(jnp.float32)), axis=1)
    right_sq = jnp.sum(jnp.square(right.astype(jnp.float32)), axis=1)
    cross = jnp.dot(left, right.T, preferred_element_type=jnp.float32)
    return jnp.exp(-(left_sq[:, None] + right_sq[None, :] - 2.0 * cross) / left.shape[1])


def close_dot(left, right):
    return jnp.dot(left, right, precision=CLOSE, preferred_element_type=jnp.float32)


def per_device(embeddings, noise, targets, level_scale, skeleton):
    leaf, width = embeddings.shape
    rank = skeleton.shape[2]
    levels = skeleton.shape[0]
    rhs = targets.shape[1]
    wide_size = lax.axis_size("wide")
    wide_bits = wide_size.bit_length() - 1
    device = lax.axis_index("narrow") * wide_size + lax.axis_index("wide")
    local_index = skeleton[:, 0, :].reshape(-1) - device * leaf
    chosen = (local_index[:, None] == jnp.arange(leaf, dtype=jnp.int32)[None, :]).astype(jnp.bfloat16)
    centers = jnp.dot(chosen, embeddings, preferred_element_type=jnp.float32)
    centers = centers.astype(jnp.bfloat16).reshape(levels, rank, width)
    for bit in range(wide_bits):
        pending = centers[bit:]
        centers = centers.at[bit:].set(pending + partner(pending, "wide", bit))
    topmost = centers[levels - 1 :]
    centers = centers.at[levels - 1 :].set(topmost + partner(topmost, "narrow", 0))
    gram = kern(embeddings, embeddings) + jnp.diag(noise)
    leaf_inverse, det_term = spd_inverse(gram)
    scales = jnp.repeat(jnp.sqrt(level_scale / rank), rank)
    bases = kern(embeddings, centers.reshape(levels * rank, width)) * scales[None, :]
    padded = jnp.pad(targets, ((0, 0), (0, LANES - rhs)))
    solved = exact_dot(leaf_inverse, jnp.concatenate([bases, padded], axis=1))
    for level in range(levels):
        start = level * rank
        base = bases[:, start : start + rank]
        part = close_dot(base.T, solved)
        summed = node_sum(part.astype(jnp.bfloat16), level + 1).astype(jnp.float32)
        cap = jnp.eye(rank, dtype=jnp.float32) + summed[:, :rank]
        cap_inverse, cap_log = spd_inverse(cap)
        coef = close_dot(cap_inverse, summed[:, rank:])
        solved = solved[:, rank:] - close_dot(solved[:, :rank], coef)
        det_term = det_term + cap_log / 2 ** (level + 1)
    answer = solved[:, :rhs]
    fit_term = jnp.sum(targets * answer, axis=0)
    totals = jnp.zeros((8, LANES), jnp.float32).at[0, :rhs].set(fit_term).at[1, 0].set(det_term)
    totals = whole_sum(totals)
    npoints = leaf * lax.axis_size("narrow") * wide_size
    return (answer, totals[0, :rhs] / npoints, totals[1, 0] / npoints)


def solution(mesh):
    return jax.shard_map(
        per_device,
        mesh=mesh,
        in_specs=(
            P(NARROW_WIDE, None),
            P(NARROW_WIDE),
            P(NARROW_WIDE, None),
            P(),
            P(None, NARROW_WIDE, None),
        ),
        out_specs=(P(NARROW_WIDE, None), P(), P()),
        check_vma=False,
    )
```

time: 992 us -> 463 us (0.47)
  other arithmetic: 480 us -> 15.1 us
  Pallas kernels: 0 us -> 296 us
  waiting for transfers between devices: 229 us -> 70.9 us
  starting transfers between devices: 89.7 us -> 18.3 us
  local copies, waits for them, and re-layouts: 72.3 us -> 15.2 us
  matrix products: 63.7 us -> 34.8 us
  blocking collectives: 28.5 us -> 0 us
    another operation x73 -> x0, other arithmetic: 444 us -> none  [the longest x48 200 us: block_cholesky(): return jnp.linalg.cholesky(matrix)]
    pallas_call x0 -> x16, Pallas kernels: none -> 296 us  [the longest x7 168 us: node_sum(): pl.pallas_call(functools.partial(node_sum_kernel, near, far), out_shape=j...]
    ppermute x35 -> x7, waiting for transfers between devices: 229 us -> 70.9 us  [partner(): return lax.ppermute(value, axis, pairs)]
    ppermute x35 -> x7, starting transfers between devices: 89.7 us -> 18.3 us  [partner(): return lax.ppermute(value, axis, pairs)]
    another operation x105 -> x0, local copies, waits for them, and re-layouts: 38.6 us -> none
    another operation x56 -> x0, matrix products: 38.4 us -> none  [the longest x42 29.8 us: per_device(): coef = jax.scipy.linalg.cho_solve((capchol, True), summed[:, rank:])]
    psum x4 -> x0, blocking collectives: 28.5 us -> none  [by_axis(): return functools.reduce(lax.psum, axes, value)]
    gather x9 -> x0, local copies, waits for them, and re-layouts: 24.5 us -> none  [the longest x7 17 us: per_device(): jnp.diagonal(capchol)]
  transfers between devices with their start and end apart: 35 -> 7, of which waited for: 28 -> 6; matrix products, arithmetic and copies ran while one was open for 9% -> 1% of each run, Pallas kernels for 0% -> 3%
where the time goes in v1:
time: 463 us; the launch traced here: 458 us
  Pallas kernels  296 us (64%)
  waiting for transfers between devices  70.9 us (15%)
  matrix products  34.8 us (8%)
  starting transfers between devices  18.3 us (4%)
  local copies, waits for them, and re-layouts  15.2 us (3%)
  other arithmetic  15.1 us (3%)
  between operations  8.18 us (2%)
    pallas_call x7, Pallas kernels, node_sum(): pl.pallas_call(functools.partial(node_sum_kernel, near, far), out_shape=j...  168 us
    pallas_call x8, Pallas kernels, spd_inverse(): pl.pallas_call(inverse_kernel, out_shape=(jax.ShapeDtypeStruct((order, or...  112 us
    ppermute x7, waiting for transfers between devices, partner(): return lax.ppermute(value, axis, pairs)  70.9 us
    dot_general x21, matrix products, close_dot(): jnp.dot(left, right, precision=CLOSE, preferred_element_type=jnp.float32)  29.9 us
    ppermute x7, starting transfers between devices, partner(): return lax.ppermute(value, axis, pairs)  18.3 us
    pallas_call x1, Pallas kernels, whole_sum(): pl.pallas_call(functools.partial(whole_sum_kernel, near, far), out_shape=...  14.8 us
    add x7, other arithmetic, per_device(): cap = jnp.eye(rank, dtype=jnp.float32) + summed[:, :rank]  11.5 us
    slice x8, local copies, waits for them, and re-layouts, spd_inverse(): return (inverse, logs[0, 0])  9.75 us
  transfers between devices with their start and end apart: 7, of which 6 were waited for; matrix products, arithmetic and copies ran while one was open for 1% of the time, Pallas kernels for 3%

profile of v1, /device:TPU:1, one launch (start us, length us, event | category | flops | bytes accessed | tf_op | source)
XLA Modules:
  0.0 458.0 jit_solution(9096205551147384155)
XLA Ops:
  2.7 2.5 collective-permute-start
  5.3 20.1 %collective-permute-done = bf16[7,256,256]{2,1,0:T(8,128)(2,1)S(1)} collective-permute-done((bf16[7,256,256]{2,1,0:T(8,128)(2,1)S(1)}, bf16[7,256,256]{2,1,0:T(8,128)(2,1)S(1)}, u32[]{:S(2)}, u32[]{:S(2)}) %collective-permute-start) | collective-permute-done | bytes 917536 | tf_op jit(solution)/shard_map/ppermute | solution.py:287
  25.7 3.2 collective-permute-start.1
  28.9 16.4 %collective-permute-done.1 = bf16[6,256,256]{2,1,0:T(8,128)(2,1)S(1)} collective-permute-done((bf16[6,256,256]{2,1,0:T(8,128)(2,1)S(1)}, bf16[6,256,256]{2,1,0:T(8,128)(2,1)S(1)}, u32[]{:S(2)}, u32[]{:S(2)}) %collective-permute-start.1) | collective-permute-done | bytes 786464 | tf_op jit(solution)/shard_map/ppermute | solution.py:287
  47.1 12.9 %collective-permute-done.2 = bf16[5,256,256]{2,1,0:T(8,128)(2,1)S(1)} collective-permute-done((bf16[5,256,256]{2,1,0:T(8,128)(2,1)S(1)}, bf16[5,256,256]{2,1,0:T(8,128)(2,1)S(1)}, u32[]{:S(2)}, u32[]{:S(2)}) %collective-permute-start.2) | collective-permute-done | bytes 655392 | tf_op jit(solution)/shard_map/ppermute | solution.py:287
  60.2 3.0 collective-permute-start.3
  63.2 10.1 %collective-permute-done.3 = bf16[4,256,256]{2,1,0:T(8,128)(2,1)S(1)} collective-permute-done((bf16[4,256,256]{2,1,0:T(8,128)(2,1)S(1)}, bf16[4,256,256]{2,1,0:T(8,128)(2,1)S(1)}, u32[]{:S(2)}, u32[]{:S(2)}) %collective-permute-start.3) | collective-permute-done | bytes 524320 | tf_op jit(solution)/shard_map/ppermute | solution.py:287
  74.9 6.1 %collective-permute-done.4 = bf16[3,256,256]{2,1,0:T(8,128)(2,1)S(1)} collective-permute-done((bf16[3,256,256]{2,1,0:T(8,128)(2,1)S(1)}, bf16[3,256,256]{2,1,0:T(8,128)(2,1)S(1)}, u32[]{:S(2)}, u32[]{:S(2)}) %collective-permute-start.4) | collective-permute-done | bytes 393248 | tf_op jit(solution)/shard_map/ppermute | solution.py:287
  81.2 2.8 collective-permute-start.5
  84.2 5.3 %collective-permute-done.5 = bf16[2,256,256]{2,1,0:T(8,128)(2,1)S(1)} collective-permute-done((bf16[2,256,256]{2,1,0:T(8,128)(2,1)S(1)}, bf16[2,256,256]{2,1,0:T(8,128)(2,1)S(1)}, u32[]{:S(2)}, u32[]{:S(2)}) %collective-permute-start.5) | collective-permute-done | bytes 262176 | tf_op jit(solution)/shard_map/ppermute | solution.py:287
  89.6 4.0 collective-permute-start.6
  94.6 13.9 %spd_inverse.8 = (f32[256,256]{1,0:T(8,128)}, f32[8,128]{1,0:T(8,128)}) custom-call(f32[256,256]{1,0:T(8,128)} %fusion.13.matrix_ref), custom_call_target="tpu_custom_call" | custom-call | flops 60000000 | bytes 600000 | tf_op jit(solution)/shard_map/spd_inverse/pallas_call | solution.py:113
  111.1 1.9 fusion.6
  113.0 2.0 convolution_convert_fusion.1.part_ref
  115.0 26.5 %node_sum_1.1 = bf16[256,1920]{1,0:T(8,128)(2,1)} custom-call(bf16[256,1920]{1,0:T(8,128)(2,1)} %convolution_convert_fusion.1.part_ref), custom_call_target="tpu_custom_call" | custom-call | tf_op jit(solution)/shard_map/node_sum_1/pallas_call | solution.py:216
  143.1 14.1 %spd_inverse.9 = (f32[256,256]{1,0:T(8,128)}, f32[8,128]{1,0:T(8,128)}) custom-call(f32[256,256]{1,0:T(8,128)} %convert_add_fusion.6.matrix_ref), custom_call_target="tpu_custom_call" | custom-call | flops 60000000 | bytes 600000 | tf_op jit(solution)/shard_map/spd_inverse/pallas_call | solution.py:113
  157.2 1.9 fusion.17
  161.4 2.9 convolution_convert_fusion.part_ref
  164.3 27.6 %node_sum_2.1 = bf16[256,1664]{1,0:T(8,128)(2,1)} custom-call(bf16[256,1664]{1,0:T(8,128)(2,1)} %convolution_convert_fusion.part_ref), custom_call_target="tpu_custom_call" | custom-call | tf_op jit(solution)/shard_map/node_sum_2/pallas_call | solution.py:216
  193.5 14.1 %spd_inverse.10 = (f32[256,256]{1,0:T(8,128)}, f32[8,128]{1,0:T(8,128)}) custom-call(f32[256,256]{1,0:T(8,128)} %convert_add_fusion.5.matrix_ref), custom_call_target="tpu_custom_call" | custom-call | flops 60000000 | bytes 600000 | tf_op jit(solution)/shard_map/spd_inverse/pallas_call | solution.py:113
  209.4 2.4 convolution_subtract_fusion.1
  213.6 22.1 %node_sum_3.1 = bf16[256,1408]{1,0:T(8,128)(2,1)} custom-call(bf16[256,1408]{1,0:T(8,128)(2,1)} %convolution_convert_fusion.4.part_ref), custom_call_target="tpu_custom_call" | custom-call | tf_op jit(solution)/shard_map/node_sum_3/pallas_call | solution.py:216
  237.3 14.3 %spd_inverse.11 = (f32[256,256]{1,0:T(8,128)}, f32[8,128]{1,0:T(8,128)}) custom-call(f32[256,256]{1,0:T(8,128)} %convert_add_fusion.4.matrix_ref), custom_call_target="tpu_custom_call" | custom-call | flops 60000000 | bytes 600000 | tf_op jit(solution)/shard_map/spd_inverse/pallas_call | solution.py:113
  256.7 24.8 %node_sum_4.1 = bf16[256,1152]{1,0:T(8,128)(2,1)} custom-call(bf16[256,1152]{1,0:T(8,128)(2,1)} %convolution_convert_fusion.3.part_ref), custom_call_target="tpu_custom_call" | custom-call | tf_op jit(solution)/shard_map/node_sum_4/pallas_call | solution.py:216
  283.1 14.0 %spd_inverse.12 = (f32[256,256]{1,0:T(8,128)}, f32[8,128]{1,0:T(8,128)}) custom-call(f32[256,256]{1,0:T(8,128)} %convert_add_fusion.3.matrix_ref), custom_call_target="tpu_custom_call" | custom-call | flops 60000000 | bytes 600000 | tf_op jit(solution)/shard_map/spd_inverse/pallas_call | solution.py:113
  302.0 22.3 %node_sum_5.1 = bf16[256,896]{1,0:T(8,128)(2,1)} custom-call(bf16[256,896]{1,0:T(8,128)(2,1)} %convolution_convert_fusion.5.part_ref), custom_call_target="tpu_custom_call" | custom-call | tf_op jit(solution)/shard_map/node_sum_5/pallas_call | solution.py:216
  325.9 14.1 %spd_inverse.13 = (f32[256,256]{1,0:T(8,128)}, f32[8,128]{1,0:T(8,128)}) custom-call(f32[256,256]{1,0:T(8,128)} %convert_add_fusion.2.matrix_ref), custom_call_target="tpu_custom_call" | custom-call | flops 60000000 | bytes 600000 | tf_op jit(solution)/shard_map/spd_inverse/pallas_call | solution.py:113
  343.2 21.4 %node_sum_6.1 = bf16[256,640]{1,0:T(8,128)(2,1)} custom-call(bf16[256,640]{1,0:T(8,128)(2,1)} %convolution_convert_fusion.6.part_ref), custom_call_target="tpu_custom_call" | custom-call | tf_op jit(solution)/shard_map/node_sum_6/pallas_call | solution.py:216
  366.3 13.8 %spd_inverse.14 = (f32[256,256]{1,0:T(8,128)}, f32[8,128]{1,0:T(8,128)}) custom-call(f32[256,256]{1,0:T(8,128)} %convert_add_fusion.1.matrix_ref), custom_call_target="tpu_custom_call" | custom-call | flops 60000000 | bytes 600000 | tf_op jit(solution)/shard_map/spd_inverse/pallas_call | solution.py:113
  390.2 23.6 %node_sum_7.1 = bf16[256,384]{1,0:T(8,128)(2,1)} custom-call(bf16[256,384]{1,0:T(8,128)(2,1)} %convolution_convert_fusion.7.part_ref), custom_call_target="tpu_custom_call" | custom-call | tf_op jit(solution)/shard_map/node_sum_7/pallas_call | solution.py:216
  415.4 14.1 %spd_inverse.15 = (f32[256,256]{1,0:T(8,128)}, f32[8,128]{1,0:T(8,128)}) custom-call(f32[256,256]{1,0:T(8,128)} %convert_add_fusion.matrix_ref), custom_call_target="tpu_custom_call" | custom-call | flops 60000000 | bytes 600000 | tf_op jit(solution)/shard_map/spd_inverse/pallas_call | solution.py:113
  438.0 14.8 %whole_sum.1 = f32[8,128]{1,0:T(8,128)} custom-call(f32[8,128]{1,0:T(8,128)} %copy-done.7), custom_call_target="tpu_custom_call" | custom-call | tf_op jit(solution)/shard_map/whole_sum/pallas_call | solution.py:265
  (87 shorter events, 56.7 us)
Async XLA Ops:
  2.7 22.6 %collective-permute-start = (bf16[7,256,256]{2,1,0:T(8,128)(2,1)S(1)}, bf16[7,256,256]{2,1,0:T(8,128)(2,1)S(1)}, u32[]{:S(2)}, u32[]{:S(2)}) collective-permute-start(bf16[7,256,256]{2,1,0:T(8,128)(2,1)S(1)} %bitcast.46), channel_id=1, source_target_pairs={{0,1},{1,0},{2,3},{3,2},{4,5},{5,4},{6,7},{7,6},{8,9},{9,8},{10,11... | collective-permute-start | bytes 2752520 | tf_op jit(solution)/shard_map/ppermute | solution.py:287
  25.7 19.6 %collective-permute-start.1 = (bf16[6,256,256]{2,1,0:T(8,128)(2,1)S(1)}, bf16[6,256,256]{2,1,0:T(8,128)(2,1)S(1)}, u32[]{:S(2)}, u32[]{:S(2)}) collective-permute-start(bf16[6,256,256]{2,1,0:T(8,128)(2,1)S(1)} %slice.427), channel_id=1, source_target_pairs={{0,2},{1,3},{2,0},{3,1},{4,6},{5,7},{6,4},{7,5},{8,10},{9,11},{10,... | collective-permute-start | bytes 2359304 | tf_op jit(solution)/shard_map/ppermute | solution.py:287
  45.8 14.3 %collective-permute-start.2 = (bf16[5,256,256]{2,1,0:T(8,128)(2,1)S(1)}, bf16[5,256,256]{2,1,0:T(8,128)(2,1)S(1)}, u32[]{:S(2)}, u32[]{:S(2)}) collective-permute-start(bf16[5,256,256]{2,1,0:T(8,128)(2,1)S(1)} %slice.428), channel_id=1, source_target_pairs={{0,4},{1,5},{2,6},{3,7},{4,0},{5,1},{6,2},{7,3},{8,12},{9,13},{10,... | collective-permute-start | bytes 1966088 | tf_op jit(solution)/shard_map/ppermute | solution.py:287
  60.2 13.1 %collective-permute-start.3 = (bf16[4,256,256]{2,1,0:T(8,128)(2,1)S(1)}, bf16[4,256,256]{2,1,0:T(8,128)(2,1)S(1)}, u32[]{:S(2)}, u32[]{:S(2)}) collective-permute-start(bf16[4,256,256]{2,1,0:T(8,128)(2,1)S(1)} %slice.429), channel_id=1, source_target_pairs={{0,8},{1,9},{2,10},{3,11},{4,12},{5,13},{6,14},{7,15},{8,0},{9,1},... | collective-permute-start | bytes 1572872 | tf_op jit(solution)/shard_map/ppermute | solution.py:287
  73.5 10.5 %copy-start.9 = (f32[7]{0:T(128)S(1)}, f32[7]{0:T(128)}, u32[]{:S(2)}) copy-start(f32[7]{0:T(128)} %param.28) | copy-start | bytes 88
  73.5 10.5 %copy-start.6 = (bf16[256,256]{1,0:T(8,128)(2,1)S(1)}, bf16[256,256]{1,0:T(8,128)(2,1)}, u32[]{:S(2)}) copy-start(bf16[256,256]{1,0:T(8,128)(2,1)} %param.25) | copy-start | bytes 393220
  73.6 20.1 %copy-start.8 = (f32[256]{0:T(256)S(1)}, f32[256]{0:T(256)}, u32[]{:S(2)}) copy-start(f32[256]{0:T(256)} %param.26) | copy-start | bytes 3076
  73.6 7.4 %collective-permute-start.4 = (bf16[3,256,256]{2,1,0:T(8,128)(2,1)S(1)}, bf16[3,256,256]{2,1,0:T(8,128)(2,1)S(1)}, u32[]{:S(2)}, u32[]{:S(2)}) collective-permute-start(bf16[3,256,256]{2,1,0:T(8,128)(2,1)S(1)} %slice.430), channel_id=1, source_target_pairs={{0,16},{1,17},{2,18},{3,19},{4,20},{5,21},{6,22},{7,23},{8,24},{9,... | collective-permute-start | bytes 1179656 | tf_op jit(solution)/shard_map/ppermute | solution.py:287
  81.1 28.5 %copy-start.4 = (f32[256,64]{0,1:T(8,128)S(1)}, f32[256,64]{0,1:T(8,128)}, u32[]{:S(2)}) copy-start(f32[256,64]{0,1:T(8,128)} %param.27) | copy-start | bytes 196612
  81.2 8.3 %collective-permute-start.5 = (bf16[2,256,256]{2,1,0:T(8,128)(2,1)S(1)}, bf16[2,256,256]{2,1,0:T(8,128)(2,1)S(1)}, u32[]{:S(2)}, u32[]{:S(2)}) collective-permute-start(bf16[2,256,256]{2,1,0:T(8,128)(2,1)S(1)} %slice.431), channel_id=1, source_target_pairs={{0,32},{1,33},{2,34},{3,35},{4,36},{5,37},{6,38},{7,39},{8,40},{9,... | collective-permute-start | bytes 786440 | tf_op jit(solution)/shard_map/ppermute | solution.py:287
  89.6 20.1 %collective-permute-start.6 = (bf16[1,256,256]{2,1,0:T(8,128)(2,1)S(1)}, bf16[1,256,256]{2,1,0:T(8,128)(2,1)S(1)}, u32[]{:S(2)}, u32[]{:S(2)}) collective-permute-start(bf16[1,256,256]{2,1,0:T(8,128)(2,1)S(1)} %slice.432), channel_id=1, source_target_pairs={{0,64},{64,0},{1,65},{65,1},{2,66},{66,2},{3,67},{67,3},{4,68},{68... | collective-permute-start | bytes 393224 | tf_op jit(solution)/shard_map/ppermute | solution.py:287
  110.1 1.0 copy-start.5
  110.8 2.2 copy-start.1
  160.2 1.2 copy-start
  209.4 2.4 copy-start.2
  254.1 1.1 copy-start.3
  437.4 0.6 copy-start.7
